TPU v7x, 32 devices: a whole 2x2x4 slice. The times are simulated.
32 devices in a mesh: seq: 8 (over y, x, core), head: 4 (over z).
Axes of the slice: x: 2, y: 2, z: 4, core: 2. Of those that a mesh axis runs over, the one named last changes fastest.
Arguments:
- mid: bfloat16 [2048, 3072], P('seq'), may hold values from -20 to 20
- second_in: bfloat16 [2048, 3072], P('seq'), may hold values from -20 to 20
- cotangent: bfloat16 [2048, 3072], P('seq'), may hold values from -6 to 6
- w_key: bfloat16 [3072, 1024], P(None, 'head'), may hold values from -0.109375 to 0.109375
- w_value: bfloat16 [3072, 1024], P(None, 'head'), may hold values from -0.109375 to 0.109375
- w_query: bfloat16 [2, 3072, 3072], P(None, None, 'head'), may hold values from -0.109375 to 0.109375
- w_out: bfloat16 [2, 3072, 3072], P(None, 'head'), may hold values from -0.109375 to 0.109375
- w_ret_out: bfloat16 [3072, 3072], P('head'), may hold values from -0.109375 to 0.109375
- ret_query: bfloat16 [2048, 3072], P('seq', 'head'), may hold values from -6 to 6
- ret_key: bfloat16 [2048, 3072], P('seq', 'head'), may hold values from -3 to 3
- ret_value: bfloat16 [2048, 3072], P('seq', 'head'), may hold values from -6 to 6
- gate: float32 [24, 2048], P('head', 'seq'), may hold values from 0 to 6
- decay_exp: int32 [24], P('head'), may hold values from 0 to 256
- mask_start: int32 [16], P('seq'), may hold values from 0 to 1920, as said below
Outputs:
- grad_mid: bfloat16 [2048, 3072], P('seq')
- grad_ret_query: bfloat16 [2048, 3072], P('seq', 'head')
- grad_ret_key: bfloat16 [2048, 3072], P('seq', 'head')
- grad_ret_value: bfloat16 [2048, 3072], P('seq', 'head')
- grad_w_key: float32 [3072, 1024], P(None, 'head')
- grad_w_value: float32 [3072, 1024], P(None, 'head')
Inputs may be any that keep to these rules, and one draw needn't show every extreme that they name: `mask_start`: the entry of each block of 128 queries is at most the position of that block's first query.
All inputs are finite; a program needn't handle non-finite values.
Results may differ from a plain program's by a relative error of at most 0.025.
The roundings to bfloat16 on the way count: a program that leaves them out, or rounds other values in their place, can miss the bound.
Values may be sent and summed in bfloat16 or wider, within the bound.
A program may use at most 192 MiB of HBM per device.

v0:
```python
import math
import jax
import jax.numpy as jnp
from jax import lax
from jax.sharding import PartitionSpec as P

E = 128
BLK = 128
RC = 128


def carried_in(value, axis, combine, identity, reverse):
    peers, position = (lax.axis_size(axis), lax.axis_index(axis))
    everything = jax.tree.map(lambda part: lax.all_gather(part, axis), value)
    start = jax.tree.map(
        lambda part, zero: jnp.broadcast_to(jnp.asarray(zero, part.dtype), part.shape),
        value,
        identity,
    )

    def lap(k, before):
        at = peers - 1 - k if reverse else k
        reached = at > position if reverse else at < position
        new = combine(before, jax.tree.map(lambda part: part[at], everything))
        return jax.tree.map(lambda a, b: jnp.where(reached, a, b), new, before)

    return lax.fori_loop(0, peers, lap, start)


def contract_last(left, right):
    return lax.dot_general(
        left, right, (((1,), (1,)), ((), ())), preferred_element_type=jnp.float32
    )


def attend_back(layer_in, w_query_l, w_out_l, upstream, keys, values, visible):
    row_count = layer_in.shape[0]
    key_count = keys.shape[0]
    kv_heads = keys.shape[1] // E
    factor = 1.0 / math.sqrt(E)
    queries = jnp.dot(layer_in, w_query_l, preferred_element_type=jnp.float32).astype(jnp.bfloat16)
    group = queries.shape[1] // keys.shape[1]
    grad_out = contract_last(upstream, w_out_l).astype(jnp.bfloat16)
    query_heads = queries.reshape(row_count, kv_heads, group, E)
    grad_heads = grad_out.reshape(row_count, kv_heads, group, E)
    key_heads = keys.reshape(key_count, kv_heads, E)
    value_heads = values.reshape(key_count, kv_heads, E)
    scores = (
        jnp.einsum("tkge,ske->kgts", query_heads, key_heads, preferred_element_type=jnp.float32)
        * factor
    )
    scores = jnp.where(visible, scores, -jnp.inf)
    top = jnp.max(scores, axis=-1, keepdims=True)
    raised = jnp.exp(scores - top)
    probs = raised / jnp.sum(raised, axis=-1, keepdims=True)
    rounded = probs.astype(jnp.bfloat16)
    outputs = jnp.einsum(
        "kgts,ske->tkge", rounded, value_heads, preferred_element_type=jnp.float32
    ).astype(jnp.bfloat16)
    delta = jnp.sum(grad_heads.astype(jnp.float32) * outputs.astype(jnp.float32), axis=-1)
    delta = jnp.transpose(delta, (1, 2, 0))[..., None]
    dprobs = jnp.einsum(
        "tkge,ske->kgts", grad_heads, value_heads, preferred_element_type=jnp.float32
    )
    dscores = (probs * (dprobs - delta) * factor).astype(jnp.bfloat16)
    query_grad = jnp.einsum(
        "kgts,ske->tkge", dscores, key_heads, preferred_element_type=jnp.float32
    )
    query_grad = query_grad.astype(jnp.bfloat16).reshape(row_count, -1)
    key_part = jnp.einsum(
        "kgts,tkge->ske", dscores, query_heads, preferred_element_type=jnp.float32
    ).reshape(key_count, -1)
    value_part = jnp.einsum(
        "kgts,tkge->ske", rounded, grad_heads, preferred_element_type=jnp.float32
    ).reshape(key_count, -1)
    return (contract_last(query_grad, w_query_l), key_part, value_part)


def retention_states(ret_key, ret_value, gate, decay_exp):
    length, width = ret_key.shape
    heads = gate.shape[0]
    size = width // heads
    count = length // RC
    key_blocks = ret_key.reshape(count, RC, heads, size)
    value_blocks = ret_value.reshape(count, RC, heads, size)
    rate = jnp.exp2(-decay_exp.astype(jnp.float32) / 64.0)
    accum = jnp.cumsum((-rate[:, None] * gate).reshape(heads, count, RC), axis=2)
    ends = accum[:, :, -1]
    shrink = jnp.transpose(jnp.exp(ends[:, :, None] - accum), (1, 2, 0))[..., None]
    weighted = (shrink * key_blocks).astype(jnp.bfloat16)
    own_state = jnp.einsum(
        "csha,cshb->hcab", weighted, value_blocks, preferred_element_type=jnp.float32
    )
    return (accum, ends, shrink, own_state)


def grad_states(ret_query, grad_o, accum):
    heads, count, block = accum.shape
    size = ret_query.shape[1] // heads
    query_blocks = ret_query.reshape(count, block, heads, size)
    grad_blocks = grad_o.reshape(count, block, heads, size)
    grow = jnp.transpose(jnp.exp(accum), (1, 2, 0))[..., None]
    weighted = (grow * query_blocks).astype(jnp.bfloat16)
    own_grad = (
        jnp.einsum("ctha,cthb->hcab", weighted, grad_blocks, preferred_element_type=jnp.float32) / E
    )
    return (grow, own_grad)


def retention_grads(ret_query, ret_key, ret_value, grad_o, accum, shrink, grow, entering, after):
    length, width = ret_query.shape
    heads, count, block = accum.shape
    size = width // heads
    shape4 = (count, block, heads, size)
    query_blocks = ret_query.reshape(shape4)
    key_blocks = ret_key.reshape(shape4)
    value_blocks = ret_value.reshape(shape4)
    grad_blocks = grad_o.reshape(shape4)
    lower = jnp.arange(block)[:, None] >= jnp.arange(block)[None, :]
    diff = accum[:, :, :, None] - accum[:, :, None, :]
    weights = jnp.where(lower, jnp.exp(jnp.where(lower, diff, 0.0)), 0.0)
    first = (
        weights
        * jnp.einsum(
            "ctha,csha->hcts", grad_blocks, value_blocks, preferred_element_type=jnp.float32
        )
    ).astype(jnp.bfloat16)
    second = (
        weights
        * jnp.einsum(
            "ctha,csha->hcts", query_blocks, key_blocks, preferred_element_type=jnp.float32
        )
    ).astype(jnp.bfloat16)
    inner_query = jnp.einsum(
        "hcts,csha->ctha", first, key_blocks, preferred_element_type=jnp.float32
    )
    inner_key = jnp.einsum(
        "hcts,ctha->csha", first, query_blocks, preferred_element_type=jnp.float32
    )
    inner_value = jnp.einsum(
        "hcts,ctha->csha", second, grad_blocks, preferred_element_type=jnp.float32
    )
    highest = lax.Precision.HIGHEST
    carried_query = jnp.einsum(
        "cthb,hcab->ctha", grad_blocks.astype(jnp.float32), entering, precision=highest
    )
    carried_key = jnp.einsum(
        "cshb,hcab->csha", value_blocks.astype(jnp.float32), after, precision=highest
    )
    carried_value = jnp.einsum(
        "csha,hcab->cshb", key_blocks.astype(jnp.float32), after, precision=highest
    )
    grad_query = (
        ((inner_query + grow * carried_query) / E).astype(jnp.bfloat16).reshape(length, width)
    )
    grad_key = (inner_key / E + shrink * carried_key).astype(jnp.bfloat16).reshape(length, width)
    grad_value = (
        (inner_value / E + shrink * carried_value).astype(jnp.bfloat16).reshape(length, width)
    )
    return (grad_query, grad_key, grad_value)


def combine_forward(earlier, later):
    return (earlier[0] * later[0], later[0] * earlier[1] + later[1])


def combine_backward(earlier, later):
    return (earlier[0] * later[0], later[1] + later[0] * earlier[1])


def head_total(partial_value, residual):
    summed = lax.psum(partial_value, "head")
    return (residual.astype(jnp.float32) + summed).astype(jnp.bfloat16)


def reduce_keys(key_part, value_part):
    return (
        lax.psum_scatter(key_part, "seq", scatter_dimension=0, tiled=True),
        lax.psum_scatter(value_part, "seq", scatter_dimension=0, tiled=True),
    )


def local(
    mid,
    second_in,
    cotangent,
    w_key,
    w_value,
    w_query,
    w_out,
    w_ret_out,
    ret_query,
    ret_key,
    ret_value,
    gate,
    decay_exp,
    mask_start,
):
    row_count = mid.shape[0]
    accum, ends, shrink, own_state = retention_states(ret_key, ret_value, gate, decay_exp)
    decay_rows = jnp.exp(ends)
    count = decay_rows.shape[1]
    device_decay = jnp.prod(decay_rows, axis=1)[:, None, None]
    device_state = jnp.zeros_like(own_state[:, 0])
    for block in range(count):
        device_state = decay_rows[:, block, None, None] * device_state + own_state[:, block]
    decay_before, incoming = carried_in(
        (device_decay, device_state),
        "seq",
        combine_forward,
        (jnp.ones_like(device_decay), jnp.zeros_like(device_state)),
        False,
    )
    keys_own = jnp.dot(mid, w_key, preferred_element_type=jnp.float32).astype(jnp.bfloat16)
    values_own = jnp.dot(mid, w_value, preferred_element_type=jnp.float32).astype(jnp.bfloat16)
    all_keys, all_values = (
        lax.all_gather(keys_own, "seq", axis=0, tiled=True),
        lax.all_gather(values_own, "seq", axis=0, tiled=True),
    )
    key_count = all_keys.shape[0]
    positions = lax.axis_index("seq") * row_count + jnp.arange(row_count, dtype=jnp.int32)
    first_seen = jnp.repeat(mask_start, BLK)
    key_positions = jnp.arange(key_count, dtype=jnp.int32)
    visible = (key_positions[None, :] >= first_seen[:, None]) & (
        key_positions[None, :] <= positions[:, None]
    )
    upper_in, upper_key, upper_value = attend_back(
        second_in, w_query[1], w_out[1], cotangent, all_keys, all_values, visible
    )
    upper_sums = reduce_keys(upper_key, upper_value)
    upstream = head_total(upper_in, cotangent)
    lower_in, lower_key, lower_value = attend_back(
        mid, w_query[0], w_out[0], upstream, all_keys, all_values, visible
    )
    lower_sums = reduce_keys(lower_key, lower_value)
    key_total = upper_sums[0] + lower_sums[0]
    value_total = upper_sums[1] + lower_sums[1]
    key_grad = key_total.astype(jnp.bfloat16)
    value_grad = value_total.astype(jnp.bfloat16)
    mid_part = lower_in + contract_last(key_grad, w_key) + contract_last(value_grad, w_value)
    grad_mid = head_total(mid_part, upstream)
    tokens_dims = (((0,), (0,)), ((), ()))
    key_weight_part = lax.dot_general(
        mid, key_grad, tokens_dims, preferred_element_type=jnp.float32
    )
    value_weight_part = lax.dot_general(
        mid, value_grad, tokens_dims, preferred_element_type=jnp.float32
    )
    grad_w_key, grad_w_value = lax.psum((key_weight_part, value_weight_part), "seq")
    grad_o = contract_last(grad_mid, w_ret_out).astype(jnp.bfloat16)
    grow, own_grad = grad_states(ret_query, grad_o, accum)
    device_grad = jnp.zeros_like(device_state)
    for block in reversed(range(count)):
        device_grad = own_grad[:, block] + decay_rows[:, block, None, None] * device_grad
    decay_after, outgoing = carried_in(
        (device_decay, device_grad),
        "seq",
        combine_backward,
        (jnp.ones_like(device_decay), jnp.zeros_like(device_grad)),
        True,
    )
    entering_list = []
    state_now = incoming
    for block in range(count):
        entering_list.append(state_now)
        state_now = decay_rows[:, block, None, None] * state_now + own_state[:, block]
    after_list = [state_now] * count
    state_now = outgoing
    for block in reversed(range(count)):
        after_list[block] = state_now
        state_now = own_grad[:, block] + decay_rows[:, block, None, None] * state_now
    entering = jnp.stack(entering_list, axis=1)
    after = jnp.stack(after_list, axis=1)
    grad_query, grad_key, grad_value = retention_grads(
        ret_query, ret_key, ret_value, grad_o, accum, shrink, grow, entering, after
    )
    return (grad_mid, grad_query, grad_key, grad_value, grad_w_key, grad_w_value)


def solution(mesh):
    placed = (
        P("seq", None),
        P("seq", None),
        P("seq", None),
        P(None, "head"),
        P(None, "head"),
        P(None, None, "head"),
        P(None, "head", None),
        P("head", None),
        P("seq", "head"),
        P("seq", "head"),
        P("seq", "head"),
        P("head", "seq"),
        P("head"),
        P("seq"),
    )
    return jax.shard_map(
        local,
        mesh=mesh,
        in_specs=placed,
        out_specs=(
            P("seq", None),
            P("seq", "head"),
            P("seq", "head"),
            P("seq", "head"),
            P(None, "head"),
            P(None, "head"),
        ),
        check_vma=False,
    )
```

profile of v0, /device:TPU:0, one launch (start us, length us, event | category | flops | bytes accessed | tf_op | source)
XLA Modules:
  0.0 662.4 jit_solution(6246297149138397294)
XLA Ops:
  7.2 1.4 copy-done
  8.6 2.6 convolution_convert_fusion.5
  11.3 2.6 convolution_convert_fusion.6
  14.0 4.3 fusion.59
  19.3 4.6 fusion.62
  23.9 1.2 copy.144
  25.2 1.3 fusion.44
  26.5 11.0 %all-gather.8.cloned.1.call-done = bf16[2048,256]{1,0:T(8,128)(2,1)} async-done(((bf16[256,256]{1,0:T(8,128)(2,1)}), bf16[2048,256]{1,0:T(8,128)(2,1)}) %all-gather.8.cloned.1.call-update) | async-done | bytes 1048592 | tf_op jit(solution)/shard_map/all_gather | solution.py:218
  37.5 2.6 reshape.147
  40.1 2.4 copy.214
  42.6 20.8 %all-gather.6.cloned.1.call-done = bf16[2048,256]{1,0:T(8,128)(2,1)} async-done(((bf16[256,256]{1,0:T(8,128)(2,1)}), bf16[2048,256]{1,0:T(8,128)(2,1)}) %all-gather.6.cloned.1.call-update) | async-done | bytes 1048592 | tf_op jit(solution)/shard_map/all_gather | solution.py:217
  63.4 2.1 reshape.145
  65.5 3.7 copy.216
  69.2 9.7 %fusion.133 = (f32[2,3,256]{2,1,0:T(4,128)S(1)}, f32[2,3,256,2048]{2,3,1,0:T(8,128)}) fusion(pred[256,2048]{0,1:T(8,128)(4,1)} %fusion.44, bf16[256,2,3,128]{0,3,2,1:T(8,128)(2,1)S(1)} %bitcast.325, bf16[2048,2,128,1]{2,1,0,3:T(2,128)(2,1)} %bitcast.312), kind=kOutput, calls=%fused_computation.176 | convolution fusion | flops 817891328 | bytes 14555136 | tf_op jit(solution)/shard_map/sub | solution.py:54
  79.0 8.2 %fusion.18 = bf16[2,3,256,2048]{2,3,1,0:T(8,128)(2,1)} fusion(f32[2,3,256,2048]{2,3,1,0:T(8,128)} %get-tuple-element.351, f32[2,3,256]{2,1,0:T(4,128)S(1)} %get-tuple-element.350), kind=kLoop, calls=%fused_computation.30 | loop fusion | flops 6291456 | bytes 18880512 | tf_op jit(solution)/shard_map/convert_element_type | solution.py:56
  87.1 3.9 fusion.77
  91.1 5.8 fusion.9
  96.9 2.6 copy-done.1
  100.6 5.5 fusion.28
  106.3 4.5 fusion.65
  110.8 1.3 copy.151
  112.0 9.9 %fusion.128 = (f32[2,3,256]{2,1,0:T(4,128)S(1)}, f32[2,3,256,2048]{2,3,1,0:T(8,128)}) fusion(pred[256,2048]{0,1:T(8,128)(4,1)} %fusion.44, bf16[256,2,3,128]{0,3,2,1:T(8,128)(2,1)S(1)} %bitcast.323, bf16[2048,2,128,1]{2,1,0,3:T(2,128)(2,1)} %bitcast.313), kind=kOutput, calls=%fused_computation.175 | convolution fusion | flops 817891328 | bytes 14555136 | tf_op jit(solution)/shard_map/sub | solution.py:54
  121.9 8.3 %fusion.19 = bf16[2,3,256,2048]{2,3,1,0:T(8,128)(2,1)} fusion(f32[2,3,256,2048]{2,3,1,0:T(8,128)} %get-tuple-element.349, f32[2,3,256]{2,1,0:T(4,128)S(1)} %get-tuple-element.348), kind=kLoop, calls=%fused_computation.31 | loop fusion | flops 6291456 | bytes 18880512 | tf_op jit(solution)/shard_map/convert_element_type | solution.py:56
  130.3 97.0 %all-reduce.6.cloned.1.call-done = f32[256,3072]{1,0:T(8,128)} async-done(((f32[256,3072]{1,0:T(8,128)}), f32[256,3072]{1,0:T(8,128)}) %all-reduce.6.cloned.1.call-update) | async-done | bytes 3145744 | tf_op jit(solution)/shard_map/psum | solution.py:172
  227.3 5.9 fusion.68
  233.2 1.2 copy.154
  234.4 3.9 fusion.78
  238.4 5.9 fusion.6
  244.3 2.1 convolution_bitcast_fusion.4
  246.5 3.5 fusion.42
  250.2 4.9 convolution_bitcast_fusion.2
  255.1 6.8 %fusion.43 = f32[2,128,2048]{2,1,0:T(8,128)} fusion(f32[2,128,2048]{2,1,0:T(8,128)S(1)} %convolution_bitcast_fusion.2, bf16[256,2,3,128]{0,3,2,1:T(8,128)(2,1)S(1)} %bitcast.319, bf16[2,3,256,2048]{2,3,1,0:T(8,128)(2,1)} %fusion.18), kind=kOutput, calls=%fused_computation.63 | convolution fusion | flops 805830656 | bytes 10878976 | tf_op jit(solution)/shard_map/kgts,tkge->ske/dot_general | solution.py:73
  262.0 3.8 convolution_convert_fusion.1
  265.8 5.6 fusion.22
  271.4 18.9 %reduce-scatter.3.cloned.1.call-done = f32[256,256]{0,1:T(8,128)} async-done(((f32[2048,256]{0,1:T(8,128)}), f32[256,256]{0,1:T(8,128)}) %reduce-scatter.3.cloned.1.call-update) | async-done | bytes 262160 | tf_op jit(solution)/shard_map/reduce_scatter | solution.py:178
  290.3 4.3 convolution_add_fusion.1
  294.5 40.0 %reduce-scatter.5.cloned.1.call-done = f32[256,256]{0,1:T(8,128)} async-done(((f32[2048,256]{0,1:T(8,128)}), f32[256,256]{0,1:T(8,128)}) %reduce-scatter.5.cloned.1.call-update) | async-done | bytes 262160 | tf_op jit(solution)/shard_map/reduce_scatter | solution.py:179
  334.5 4.7 convolution_add_fusion
  339.5 1.8 reduce_window_sum.13
  347.7 3.2 convolution_bitcast_fusion.1
  350.9 2.2 convolution_bitcast_fusion
  354.9 105.6 %all-reduce.8.cloned.1.call-done = f32[256,3072]{1,0:T(8,128)} async-done(((f32[256,3072]{1,0:T(8,128)}), f32[256,3072]{1,0:T(8,128)}) %all-reduce.8.cloned.1.call-update) | async-done | bytes 3145744 | tf_op jit(solution)/shard_map/psum | solution.py:172
  460.5 4.0 add_convert_fusion
  465.7 3.8 convolution_convert_fusion
  471.7 1.5 fusion.98
  473.3 1.3 dynamic-slice
  475.7 1.3 dynamic-update-slice
  477.0 14.7 %all-reduce = f32[48]{0:T(128)} all-reduce(f32[48]{0:T(128)} %dynamic-update-slice), channel_id=2, replica_groups=mesh['seq'=8,'head'=4] {'seq'}, use_global_device_ids=true, to_apply=%add | all-reduce | flops 48 | bytes 384
  491.7 1.3 reshape.165
  493.7 2.3 fusion.58
  496.0 18.2 %while.30 = (s32[]{:T(128)}, f32[6,128,128]{2,1,0:T(8,128)S(1)}, s32[]{:T(128)}, f32[8,6,1,1]{1,3,2,0:T(1,128)}, f32[8,6,128,128]{3,2,1,0:T(8,128)}, /*index=5*/s32[]{:T(128)}, s32[]{:T(128)}) while((s32[]{:T(128)}, f32[6,128,128]{2,1,0:T(8,128)S(1)}, s32[]{:T(128)}, f32[8,6,1,1]{1,3,2,0:T(1,128)}, ...), condition=%wide.region_15.16_spmd.clone, body=%wide.region_14.15_spmd.clone.sunk | while | flops 393220 | bytes 1179825 | solution.py:27
  502.8 1.2 dynamic-slice_bitcast_fusion.4
  503.9 1.1 fusion.184
  507.3 1.2 dynamic-slice_bitcast_fusion.4
  509.6 1.1 dynamic-slice_bitcast_fusion.4
  514.2 1.9 fusion.102
  516.0 86.0 %all-reduce.10.cloned.1.call-done = (f32[3072,256]{0,1:T(8,128)}, f32[3072,256]{0,1:T(8,128)}) async-done(((f32[3072,256]{0,1:T(8,128)}, f32[3072,256]{0,1:T(8,128)}), (f32[3072,256]{0,1:T(8,128)}, f32[3072,256]{0,1:T(8,128)})) %all-reduce.10.cloned.1.call-update) | async-done | bytes 6291472 | tf_op jit(solution)/shard_map/psum | solution.py:249
  602.1 3.5 copy.208
  605.6 3.5 copy.209
  609.2 2.0 fusion.49
  611.1 1.6 fusion.57
  614.2 22.0 %all-gather.12.cloned.1.call-done = f32[8,6,128,128]{3,2,1,0:T(8,128)} async-done(((f32[1,6,128,128]{3,2,1,0:T(8,128)}), f32[8,6,128,128]{3,2,1,0:T(8,128)}) %all-gather.12.cloned.1.call-update) | async-done | bytes 3145744 | tf_op jit(solution)/shard_map/all_gather | solution.py:14
  636.3 14.1 %while.31 = (s32[]{:T(128)}, f32[6,128,128]{2,1,0:T(8,128)S(1)}, s32[]{:T(128)}, f32[8,6,128,128]{3,2,1,0:T(8,128)}, f32[8,6,1,1]{1,3,2,0:T(1,128)}, /*index=5*/s32[]{:T(128)}, s32[]{:T(128)}, s32[]{:T(128)}, s32[]{:T(128)}) while((s32[]{:T(128)}, f32[6,128,128]{2,1,0:T(8,128)S(1)}, s32[]{:T(128)}, ...), condition=%wide.region_17.18_spmd.clone, body=%wide.region_16.17_spmd.clone.sunk | while | flops 393224 | bytes 1179887 | solution.py:27
  650.5 1.2 fusion.101
  (169 shorter events, 48.3 us)
Async XLA Ops:
  7.2 1.4 copy-start
  7.2 30.4 %all-gather.8.cloned.1.call-start = ((), (), s32[]{:S(2)}) async-start(), calls=%async_computation.3 | async-start | bytes 1179648 | tf_op jit(solution)/shard_map/all_gather | solution.py:218
  11.2 52.2 %all-gather.6.cloned.1.call-start = ((), (), s32[]{:S(2)}) async-start(), calls=%async_computation.2 | async-start | bytes 1179648 | tf_op jit(solution)/shard_map/all_gather | solution.py:217
  13.9 213.3 %all-reduce.6.cloned.1.call-start = ((), (), s32[]{:S(2)}) async-start(), calls=%async_computation.4 | async-start | bytes 6291456 | tf_op jit(solution)/shard_map/psum | solution.py:172
  14.0 5.2 copy-start.13
  19.2 5.8 copy-start.35
  23.9 45.4 %copy-start.22 = (bf16[256,768]{0,1:T(8,128)(2,1)S(1)}, bf16[256,768]{0,1:T(8,128)(2,1)}, u32[]{:S(2)}) copy-start(bf16[256,768]{0,1:T(8,128)(2,1)} %copy.141) | copy-start | bytes 1179652
  87.1 3.9 copy-start.7
  91.0 8.5 %copy-start.3 = (bf16[2048,2,128,1]{0,2,3,1:T(8,128)(2,1)S(1)}, bf16[2048,2,128,1]{0,2,3,1:T(8,128)(2,1)}, u32[]{:S(2)}) copy-start(bf16[2048,2,128,1]{0,2,3,1:T(8,128)(2,1)} %copy.216) | copy-start | bytes 3145732
  96.9 2.7 copy-start.1
  106.1 184.2 %reduce-scatter.3.cloned.1.call-start = ((), (), s32[]{:S(2)}) async-start(), calls=%async_computation.8 | async-start | bytes 2359296 | tf_op jit(solution)/shard_map/reduce_scatter | solution.py:178
  112.0 9.9 %copy-start.11 = (bf16[256,768]{0,1:T(8,128)(2,1)}, bf16[256,768]{0,1:T(8,128)(2,1)S(1)}, u32[]{:S(2)}) copy-start(bf16[256,768]{0,1:T(8,128)(2,1)S(1)} %copy.151) | copy-start | bytes 1179652
  234.4 4.0 copy-start.8
  234.4 12.0 %slice-start = ((s8[6291456]{0:T(1024)(128)(4,1)}), s8[4194304]{0:T(1024)(128)(4,1)S(1)}, s32[]{:S(2)}) async-start(s8[6291456]{0:T(1024)(128)(4,1)} %bitcast.301), calls=%async_computation.11 | async-start | bytes 8388608
  238.3 5.9 copy-start.12
  238.4 8.1 %slice-start.1 = ((s8[6291456]{0:T(1024)(128)(4,1)}), s8[2097152]{0:T(1024)(128)(4,1)S(1)}, s32[]{:S(2)}) async-start(s8[6291456]{0:T(1024)(128)(4,1)} %bitcast.301), calls=%async_computation.12 | async-start | bytes 4194304
  244.3 5.6 copy-start.2
  244.3 2.1 copy-start.23
  249.9 84.6 %reduce-scatter.5.cloned.1.call-start = ((), (), s32[]{:S(2)}) async-start(), calls=%async_computation.9 | async-start | bytes 2359296 | tf_op jit(solution)/shard_map/reduce_scatter | solution.py:179
  255.1 6.9 %copy-start.4 = (bf16[2048,2,128,1]{0,2,3,1:T(8,128)(2,1)S(1)}, bf16[2048,2,128,1]{0,2,3,1:T(8,128)(2,1)}, u32[]{:S(2)}) copy-start(bf16[2048,2,128,1]{0,2,3,1:T(8,128)(2,1)} %copy.216) | copy-start | bytes 3145732
  261.9 198.6 %all-reduce.8.cloned.1.call-start = ((), (), s32[]{:S(2)}) async-start(), calls=%async_computation.5 | async-start | bytes 6291456 | tf_op jit(solution)/shard_map/psum | solution.py:172
  265.8 24.4 %copy-start.19 = (bf16[3072,256]{1,0:T(8,128)(2,1)S(1)}, bf16[3072,256]{1,0:T(8,128)(2,1)}, u32[]{:S(2)}) copy-start(bf16[3072,256]{1,0:T(8,128)(2,1)} %param.21) | copy-start | bytes 4718596
  294.5 44.8 %copy-start.36 = (s32[6]{0:T(128)S(1)}, s32[6]{0:T(128)}, u32[]{:S(2)}) copy-start(s32[6]{0:T(128)} %param.30) | copy-start | bytes 76
  294.5 44.8 %copy-start.32 = (f32[6,256]{1,0:T(8,128)S(1)}, f32[6,256]{1,0:T(8,128)}, u32[]{:S(2)}) copy-start(f32[6,256]{1,0:T(8,128)} %param.29) | copy-start | bytes 18436
  294.5 47.6 %copy-start.25 = (bf16[256,768]{1,0:T(8,128)(2,1)S(1)}, bf16[256,768]{1,0:T(8,128)(2,1)}, u32[]{:S(2)}) copy-start(bf16[256,768]{1,0:T(8,128)(2,1)} %param.28) | copy-start | bytes 1179652
  339.3 3.6 copy-start.26
  339.3 156.7 %all-gather.10.cloned.1.call-start = ((), (), s32[]{:S(2)}) async-start(), calls=%async_computation.6 | async-start | bytes 3538944 | tf_op jit(solution)/shard_map/all_gather | solution.py:14
  341.3 0.9 copy-start.29
  342.9 8.0 %copy-start.17 = (bf16[2,128,6,128]{3,1,0,2:T(8,128)(2,1)}, bf16[2,128,6,128]{3,1,0,2:T(8,128)(2,1)S(1)}, u32[]{:S(2)}) copy-start(bf16[2,128,6,128]{3,1,0,2:T(8,128)(2,1)S(1)} %copy.168) | copy-start | bytes 1179652
  343.2 10.0 %copy-start.15 = (bf16[2,128,6,128]{1,0,3,2:T(2,128)(2,1)}, bf16[2,128,6,128]{1,0,3,2:T(2,128)(2,1)S(1)}, u32[]{:S(2)}) copy-start(bf16[2,128,6,128]{1,0,3,2:T(2,128)(2,1)S(1)} %reshape.160) | copy-start | bytes 1179652
  343.2 7.7 %copy-start.24 = (f32[256,256]{0,1:T(8,128)S(1)}, f32[256,256]{0,1:T(8,128)}, u32[]{:S(2)}) copy-start(f32[256,256]{0,1:T(8,128)} %reduce-scatter.5.cloned.1.call-done) | copy-start | bytes 786436
  344.8 6.2 copy-start.33
  345.9 0.9 copy-start.6
  347.7 254.4 %all-reduce.10.cloned.1.call-start = ((), (), s32[]{:S(2)}) async-start(), calls=%async_computation.10 | async-start | bytes 12582912 | tf_op jit(solution)/shard_map/psum | solution.py:249
  353.2 0.7 copy-start.30
  353.2 1.0 copy-start.27
  353.2 283.1 %all-gather.12.cloned.1.call-start = ((), (), s32[]{:S(2)}) async-start(), calls=%async_computation.7 | async-start | bytes 3538944 | tf_op jit(solution)/shard_map/all_gather | solution.py:14
  354.5 110.0 %copy-start.16 = (bf16[2,128,6,128]{1,0,3,2:T(2,128)(2,1)}, bf16[2,128,6,128]{1,0,3,2:T(2,128)(2,1)S(1)}, u32[]{:S(2)}) copy-start(bf16[2,128,6,128]{1,0,3,2:T(2,128)(2,1)S(1)} %reshape.162) | copy-start | bytes 1179652
  354.9 115.3 %copy-start.9 = (bf16[2,128,6,128]{3,1,2,0:T(8,128)(2,1)}, bf16[2,128,6,128]{3,1,2,0:T(8,128)(2,1)S(1)}, u32[]{:S(2)}) copy-start(bf16[2,128,6,128]{3,1,2,0:T(8,128)(2,1)S(1)} %copy.186) | copy-start | bytes 1179652
  464.5 1.1 copy-start.14
  470.2 3.0 copy-start.18
  470.8 0.9 copy-start.5
  493.1 0.6 copy-start.31
  612.7 0.7 copy-start.20
  612.7 37.8 %copy-start.34 = (f32[6]{0:T(128)S(1)}, f32[6]{0:T(128)}, u32[]{:S(2)}) copy-start(f32[6]{0:T(128)} %copy-done.33) | copy-start | bytes 76
  636.3 16.9 %copy-start.10 = (bf16[2,128,6,128]{3,1,2,0:T(8,128)(2,1)S(1)}, bf16[2,128,6,128]{3,1,2,0:T(8,128)(2,1)}, u32[]{:S(2)}) copy-start(bf16[2,128,6,128]{3,1,2,0:T(8,128)(2,1)} %copy-done.9) | copy-start | bytes 1179652
  650.5 2.8 copy-start.21
  650.5 3.4 copy-start.28
Sparse Core Ops, SparseCore 0:
  11.4 26.1 all-gather.7
  40.0 23.3 all-gather.5
  106.2 121.0 all-reduce.5
  250.1 40.1 reduce-scatter.2
  293.4 41.1 reduce-scatter.4
  339.4 121.0 all-reduce.7
  463.0 31.3 all-gather.9
  498.2 103.8 all-reduce.9
  604.0 32.2 all-gather.11
where the time goes:
time: 668 us; the launch traced here: 662 us
  waiting for transfers between devices  402 us (60%)
  matrix products  125 us (19%)
  local copies, waits for them, and re-layouts  56 us (8%)
  other arithmetic  48.8 us (7%)
  between operations  15.5 us (2%)
  blocking collectives  14.7 us (2%)
    psum x2, waiting for transfers between devices, head_total(): summed = lax.psum(partial_value, 'head')  203 us
    psum x1, waiting for transfers between devices, local(): lax.psum((key_weight_part, value_weight_part), 'seq')  86 us
    reduce_scatter x1, waiting for transfers between devices, reduce_keys(): lax.psum_scatter(value_part, 'seq', scatter_dimension=0, tiled=True)  40 us
    dot_general x7, matrix products, contract_last(): lax.dot_general(left, right, (((1,), (1,)), ((), ())), preferred_element_...  34.4 us
    all_gather x2, waiting for transfers between devices, carried_in(): everything = jax.tree.map(lambda part: lax.all_gather(part, axis), value)  22 us
    unnamed x91, local copies, waits for them, and re-layouts  21.9 us
    all_gather x1, waiting for transfers between devices, local(): lax.all_gather(keys_own, 'seq', axis=0, tiled=True)  20.8 us
    sub x2, matrix products, attend_back(): raised = jnp.exp(scores - top)  19.6 us
  transfers between devices with their start and end apart: 9, of which 8 were waited for; matrix products, arithmetic and copies ran while one was open for 20% of the time, Pallas kernels for 0%

commit v1 on v0

--- a/solution.py
+++ b/solution.py
@@ -169,7 +169,9 @@
 
 
 def head_total(partial_value, residual):
-    summed = lax.psum(partial_value, "head")
+    summed = partial_value
+    for hop in (1, 2):
+        summed = summed + lax.ppermute(summed, "head", [(dev, dev ^ hop) for dev in range(4)])
     return (residual.astype(jnp.float32) + summed).astype(jnp.bfloat16)
 
 

time: 668 us -> 741 us (1.11)
  waiting for transfers between devices: 402 us -> 456 us
  local copies, waits for them, and re-layouts: 56 us -> 64.6 us
  matrix products: 125 us -> 117 us
  starting transfers between devices: 1.01 us -> 8.49 us
    ppermute x0 -> x4, waiting for transfers between devices: none -> 375 us  [head_total(): lax.ppermute(summed, 'head', [(dev, dev ^ hop) for dev in range(4)])]
    psum x2 -> x0, waiting for transfers between devices: 203 us -> none  [head_total(): summed = lax.psum(partial_value, 'head')]
    psum x1, waiting for transfers between devices: 86 us -> 0.01 us  [local(): lax.psum((key_weight_part, value_weight_part), 'seq')]
    all_gather x2, waiting for transfers between devices: 22 us -> 0.01 us  [carried_in(): everything = jax.tree.map(lambda part: lax.all_gather(part, axis), value)]
    reduce_scatter x1, waiting for transfers between devices: 18.9 us -> 7.27 us  [reduce_keys(): lax.psum_scatter(key_part, 'seq', scatter_dimension=0, tiled=True)]
    ppermute x0 -> x4, starting transfers between devices: none -> 7.95 us  [head_total(): lax.ppermute(summed, 'head', [(dev, dev ^ hop) for dev in range(4)])]
    unnamed x91 -> x101, local copies, waits for them, and re-layouts: 21.9 us -> 24.6 us
  transfers between devices with their start and end apart: 9 -> 11, of which waited for: 8 -> 8; matrix products, arithmetic and copies ran while one was open for 20% -> 19% of each run, Pallas kernels for 0% -> 0%
where the time goes in v1:
time: 741 us; the launch traced here: 731 us
  waiting for transfers between devices  456 us (62%)
  matrix products  117 us (16%)
  local copies, waits for them, and re-layouts  64.6 us (9%)
  other arithmetic  55.5 us (7%)
  between operations  16 us (2%)
  blocking collectives  13.3 us (2%)
  starting transfers between devices  8.49 us (1%)
    ppermute x4, waiting for transfers between devices, head_total(): lax.ppermute(summed, 'head', [(dev, dev ^ hop) for dev in range(4)])  375 us
    reduce_scatter x1, waiting for transfers between devices, reduce_keys(): lax.psum_scatter(value_part, 'seq', scatter_dimension=0, tiled=True)  40 us
    dot_general x7, matrix products, contract_last(): lax.dot_general(left, right, (((1,), (1,)), ((), ())), preferred_element_...  29.8 us
    unnamed x101, local copies, waits for them, and re-layouts  24.6 us
    all_gather x1, waiting for transfers between devices, local(): lax.all_gather(keys_own, 'seq', axis=0, tiled=True)  21.2 us
    sub x2, matrix products, attend_back(): raised = jnp.exp(scores - top)  19.7 us
    select_n x16, other arithmetic, lap(): return jax.tree.map(lambda a, b: jnp.where(reached, a, b), new, before)  17.8 us
    convert_element_type x2, other arithmetic, attend_back(): rounded = probs.astype(jnp.bfloat16)  16.6 us
  transfers between devices with their start and end apart: 11, of which 8 were waited for; matrix products, arithmetic and copies ran while one was open for 19% of the time, Pallas kernels for 0%

profile of v1, /device:TPU:0, one launch (start us, length us, event | category | flops | bytes accessed | tf_op | source)
XLA Modules:
  0.0 730.8 jit_solution(14714444197125903966)
XLA Ops:
  7.2 1.3 copy-done
  8.6 2.6 convolution_convert_fusion.5
  12.6 4.3 fusion.59
  17.9 4.5 fusion.62
  23.6 1.3 fusion.44
  25.0 12.5 %all-gather.8.cloned.1.call-done = bf16[2048,256]{1,0:T(8,128)(2,1)} async-done(((bf16[256,256]{1,0:T(8,128)(2,1)}), bf16[2048,256]{1,0:T(8,128)(2,1)}) %all-gather.8.cloned.1.call-update) | async-done | bytes 1048592 | tf_op jit(solution)/shard_map/all_gather | solution.py:220
  37.5 2.1 reshape.147
  39.6 2.5 copy.214
  42.1 21.2 %all-gather.6.cloned.1.call-done = bf16[2048,256]{1,0:T(8,128)(2,1)} async-done(((bf16[256,256]{1,0:T(8,128)(2,1)}), bf16[2048,256]{1,0:T(8,128)(2,1)}) %all-gather.6.cloned.1.call-update) | async-done | bytes 1048592 | tf_op jit(solution)/shard_map/all_gather | solution.py:219
  63.4 2.1 reshape.145
  65.5 3.7 copy.216
  69.2 9.8 %fusion.131 = (f32[2,3,256]{2,1,0:T(4,128)S(1)}, f32[2,3,256,2048]{2,3,1,0:T(8,128)}) fusion(pred[256,2048]{0,1:T(8,128)(4,1)} %fusion.44, bf16[256,2,3,128]{0,3,2,1:T(8,128)(2,1)S(1)} %bitcast.322, bf16[2048,2,128,1]{2,1,0,3:T(2,128)(2,1)} %bitcast.309), kind=kOutput, calls=%fused_computation.175 | convolution fusion | flops 817891328 | bytes 14555136 | tf_op jit(solution)/shard_map/sub | solution.py:54
  79.0 8.2 %fusion.18 = bf16[2,3,256,2048]{2,3,1,0:T(8,128)(2,1)} fusion(f32[2,3,256,2048]{2,3,1,0:T(8,128)} %get-tuple-element.351, f32[2,3,256]{2,1,0:T(4,128)S(1)} %get-tuple-element.350), kind=kLoop, calls=%fused_computation.30 | loop fusion | flops 6291456 | bytes 18880512 | tf_op jit(solution)/shard_map/convert_element_type | solution.py:56
  87.2 3.9 fusion.76
  91.1 6.0 fusion.9
  98.1 1.6 copy-done.2
  99.8 3.9 fusion.28
  103.7 1.5 collective-permute-start
  105.2 68.8 %collective-permute-done = f32[256,3072]{1,0:T(8,128)S(1)} collective-permute-done((f32[256,3072]{1,0:T(8,128)S(1)}, f32[256,3072]{1,0:T(8,128)S(1)}, u32[]{:S(2)}, u32[]{:S(2)}) %collective-permute-start) | collective-permute-done | bytes 3145760 | tf_op jit(solution)/shard_map/ppermute | solution.py:174
  174.0 2.2 add.179
  176.2 2.4 collective-permute-start.1
  178.6 2.1 fusion.65
  181.9 9.9 %fusion.126 = (f32[2,3,256]{2,1,0:T(4,128)S(1)}, f32[2,3,256,2048]{2,3,1,0:T(8,128)}) fusion(pred[256,2048]{0,1:T(8,128)(4,1)} %fusion.44, bf16[256,2,3,128]{0,3,2,1:T(8,128)(2,1)S(1)} %bitcast.320, bf16[2048,2,128,1]{2,1,0,3:T(2,128)(2,1)} %bitcast.310), kind=kOutput, calls=%fused_computation.174 | convolution fusion | flops 817891328 | bytes 14555136 | tf_op jit(solution)/shard_map/sub | solution.py:54
  191.8 8.4 %fusion.19 = bf16[2,3,256,2048]{2,3,1,0:T(8,128)(2,1)} fusion(f32[2,3,256,2048]{2,3,1,0:T(8,128)} %get-tuple-element.349, f32[2,3,256]{2,1,0:T(4,128)S(1)} %get-tuple-element.348), kind=kLoop, calls=%fused_computation.31 | loop fusion | flops 6291456 | bytes 18880512 | tf_op jit(solution)/shard_map/convert_element_type | solution.py:56
  200.2 114.0 %collective-permute-done.1 = f32[256,3072]{1,0:T(8,128)} collective-permute-done((f32[256,3072]{1,0:T(8,128)}, f32[256,3072]{1,0:T(8,128)}, u32[]{:S(2)}, u32[]{:S(2)}) %collective-permute-start.1) | collective-permute-done | bytes 3145760 | tf_op jit(solution)/shard_map/ppermute | solution.py:174
  314.2 3.6 add_convert_fusion.1
  318.9 4.5 fusion.68
  324.7 4.2 multiply_reduce_fusion
  328.9 5.9 fusion.6
  334.8 2.1 convolution_bitcast_fusion.4
  337.5 3.5 fusion.42
  341.0 4.9 convolution_bitcast_fusion.2
  346.0 6.5 fusion.43
  352.7 1.8 reduce_window_sum.13
  358.8 1.3 copy.171
  361.7 1.6 fusion.103
  365.4 3.8 convolution_convert_fusion.1
  369.3 5.6 fusion.22
  375.0 7.3 reduce-scatter.3.cloned.1.call-done
  382.2 4.3 convolution_add_fusion.1
  386.5 40.0 %reduce-scatter.5.cloned.1.call-done = f32[256,256]{0,1:T(8,128)} async-done(((f32[2048,256]{0,1:T(8,128)}), f32[256,256]{0,1:T(8,128)}) %reduce-scatter.5.cloned.1.call-update) | async-done | bytes 262160 | tf_op jit(solution)/shard_map/reduce_scatter | solution.py:181
  426.5 3.1 convolution_add_fusion
  429.6 1.6 collective-permute-start.2
  431.2 68.2 %collective-permute-done.2 = f32[256,3072]{1,0:T(8,128)S(1)} collective-permute-done((f32[256,3072]{1,0:T(8,128)S(1)}, f32[256,3072]{1,0:T(8,128)S(1)}, u32[]{:S(2)}, u32[]{:S(2)}) %collective-permute-start.2) | collective-permute-done | bytes 3145760 | tf_op jit(solution)/shard_map/ppermute | solution.py:174
  499.4 2.2 add.186
  501.5 2.4 collective-permute-start.3
  504.0 2.3 convolution_bitcast_fusion
  506.2 2.2 convolution_bitcast_fusion.1
  509.3 1.9 copy.184
  511.3 1.9 reshape.162
  513.2 1.9 copy.186
  515.1 123.8 %collective-permute-done.3 = f32[256,3072]{1,0:T(8,128)} collective-permute-done((f32[256,3072]{1,0:T(8,128)}, f32[256,3072]{1,0:T(8,128)}, u32[]{:S(2)}, u32[]{:S(2)}) %collective-permute-start.3) | collective-permute-done | bytes 3145760 | tf_op jit(solution)/shard_map/ppermute | solution.py:174
  639.0 3.6 add_convert_fusion
  643.7 3.8 convolution_convert_fusion
  654.4 13.3 %all-reduce = f32[48]{0:T(128)} all-reduce(f32[48]{0:T(128)} %dynamic-update-slice), channel_id=2, replica_groups=mesh['seq'=8,'head'=4] {'seq'}, use_global_device_ids=true, to_apply=%add | all-reduce | flops 48 | bytes 384
  667.7 1.3 reshape.165
  669.6 2.3 fusion.58
  671.9 18.2 %while.30 = (s32[]{:T(128)}, f32[6,128,128]{2,1,0:T(8,128)S(1)}, s32[]{:T(128)}, f32[8,6,1,1]{1,3,2,0:T(1,128)}, f32[8,6,128,128]{3,2,1,0:T(8,128)}, /*index=5*/s32[]{:T(128)}, s32[]{:T(128)}) while((s32[]{:T(128)}, f32[6,128,128]{2,1,0:T(8,128)S(1)}, s32[]{:T(128)}, f32[8,6,1,1]{1,3,2,0:T(1,128)}, ...), condition=%wide.region_13.14_spmd.clone, body=%wide.region_12.13_spmd.clone.sunk | while | flops 393220 | bytes 1179825 | solution.py:27
  690.1 1.9 fusion.100
  692.0 3.5 copy.208
  695.5 3.5 copy.209
  699.0 2.0 fusion.49
  701.0 1.5 fusion.57
  704.1 14.2 %while.31 = (s32[]{:T(128)}, f32[6,128,128]{2,1,0:T(8,128)S(1)}, s32[]{:T(128)}, f32[8,6,128,128]{3,2,1,0:T(8,128)}, f32[8,6,1,1]{1,3,2,0:T(1,128)}, /*index=5*/s32[]{:T(128)}, s32[]{:T(128)}, s32[]{:T(128)}, s32[]{:T(128)}) while((s32[]{:T(128)}, f32[6,128,128]{2,1,0:T(8,128)S(1)}, s32[]{:T(128)}, ...), condition=%wide.region_15.16_spmd.clone, body=%wide.region_14.15_spmd.clone.sunk | while | flops 393224 | bytes 1179887 | solution.py:27
  (185 shorter events, 64.2 us)
Async XLA Ops:
  7.2 1.4 copy-start
  7.2 4.1 copy-start.20
  7.2 30.3 %all-gather.8.cloned.1.call-start = ((), (), s32[]{:S(2)}) async-start(), calls=%async_computation.3 | async-start | bytes 1179648 | tf_op jit(solution)/shard_map/all_gather | solution.py:220
  11.2 52.1 %all-gather.6.cloned.1.call-start = ((), (), s32[]{:S(2)}) async-start(), calls=%async_computation.2 | async-start | bytes 1179648 | tf_op jit(solution)/shard_map/all_gather | solution.py:219
  12.5 369.7 %reduce-scatter.3.cloned.1.call-start = ((), (), s32[]{:S(2)}) async-start(), calls=%async_computation.6 | async-start | bytes 2359296 | tf_op jit(solution)/shard_map/reduce_scatter | solution.py:180
  12.6 5.3 copy-start.16
  17.9 5.7 copy-start.37
  39.6 29.6 %copy-start.24 = (bf16[256,768]{0,1:T(8,128)(2,1)S(1)}, bf16[256,768]{0,1:T(8,128)(2,1)}, u32[]{:S(2)}) copy-start(bf16[256,768]{0,1:T(8,128)(2,1)} %copy.141) | copy-start | bytes 1179652
  87.2 3.9 copy-start.9
  91.1 6.0 copy-start.3
  97.1 2.7 copy-start.2
  99.8 78.8 %slice-start.2 = ((s8[9437184]{0:T(1024)(128)(4,1)}), s8[4194304]{0:T(1024)(128)(4,1)S(1)}, s32[]{:S(2)}) async-start(s8[9437184]{0:T(1024)(128)(4,1)} %bitcast.331), calls=%async_computation.11 | async-start | bytes 8388608
  99.8 78.8 %slice-start.3 = ((s8[9437184]{0:T(1024)(128)(4,1)}), s8[4194304]{0:T(1024)(128)(4,1)S(1)}, s32[]{:S(2)}) async-start(s8[9437184]{0:T(1024)(128)(4,1)} %bitcast.331), calls=%async_computation.12 | async-start | bytes 8388608
  103.7 74.9 %slice-start.4 = ((s8[9437184]{0:T(1024)(128)(4,1)}), s8[1048576]{0:T(1024)(128)(4,1)S(1)}, s32[]{:S(2)}) async-start(s8[9437184]{0:T(1024)(128)(4,1)} %bitcast.331), calls=%async_computation.13 | async-start | bytes 2097152
  103.7 70.3 %collective-permute-start = (f32[256,3072]{1,0:T(8,128)S(1)}, f32[256,3072]{1,0:T(8,128)S(1)}, u32[]{:S(2)}, u32[]{:S(2)}) collective-permute-start(f32[256,3072]{1,0:T(8,128)S(1)} %fusion.28), channel_id=1, source_target_pairs={{0,1},{1,0},{2,3},{3,2},{4,5},{5,4},{6,7},{7,6},{8,9},{9,8},{10,11... | collective-permute-start | bytes 9437192 | tf_op jit(solution)/shard_map/ppermute | solution.py:174
  176.2 138.0 %collective-permute-start.1 = (f32[256,3072]{1,0:T(8,128)}, f32[256,3072]{1,0:T(8,128)}, u32[]{:S(2)}, u32[]{:S(2)}) collective-permute-start(f32[256,3072]{1,0:T(8,128)} %add.179), channel_id=1, source_target_pairs={{0,2},{1,3},{2,0},{3,1},{4,6},{5,7},{6,4},{7,5},{8,10},{9,11},{10,... | collective-permute-start | bytes 9437192 | tf_op jit(solution)/shard_map/ppermute | solution.py:174
  181.9 9.9 %copy-start.14 = (bf16[256,768]{0,1:T(8,128)(2,1)}, bf16[256,768]{0,1:T(8,128)(2,1)S(1)}, u32[]{:S(2)}) copy-start(bf16[256,768]{0,1:T(8,128)(2,1)S(1)} %copy.151) | copy-start | bytes 1179652
  191.8 122.4 %copy-start.17 = (bf16[256,3072]{1,0:T(8,128)(2,1)S(1)}, bf16[256,3072]{1,0:T(8,128)(2,1)}, u32[]{:S(2)}) copy-start(bf16[256,3072]{1,0:T(8,128)(2,1)} %param.20) | copy-start | bytes 4718596
  317.8 1.1 copy-start.5
  324.7 4.2 copy-start.10
  324.7 12.8 %slice-start = ((s8[6291456]{0:T(1024)(128)(4,1)}), s8[4194304]{0:T(1024)(128)(4,1)S(1)}, s32[]{:S(2)}) async-start(s8[6291456]{0:T(1024)(128)(4,1)} %bitcast.298), calls=%async_computation.9 | async-start | bytes 8388608
  328.9 5.9 copy-start.15
  328.9 8.6 %slice-start.1 = ((s8[6291456]{0:T(1024)(128)(4,1)}), s8[2097152]{0:T(1024)(128)(4,1)S(1)}, s32[]{:S(2)}) async-start(s8[6291456]{0:T(1024)(128)(4,1)} %bitcast.298), calls=%async_computation.10 | async-start | bytes 4194304
  334.8 2.7 copy-start.1
  334.8 2.7 copy-start.25
  341.0 85.5 %reduce-scatter.5.cloned.1.call-start = ((), (), s32[]{:S(2)}) async-start(), calls=%async_computation.7 | async-start | bytes 2359296 | tf_op jit(solution)/shard_map/reduce_scatter | solution.py:181
  345.9 6.7 copy-start.38
  346.0 6.7 copy-start.32
  346.0 9.4 %copy-start.28 = (bf16[256,768]{1,0:T(8,128)(2,1)S(1)}, bf16[256,768]{1,0:T(8,128)(2,1)}, u32[]{:S(2)}) copy-start(bf16[256,768]{1,0:T(8,128)(2,1)} %param.28) | copy-start | bytes 1179652
  352.5 319.4 %all-gather.10.cloned.1.call-start = ((), (), s32[]{:S(2)}) async-start(), calls=%async_computation.4 | async-start | bytes 3538944 | tf_op jit(solution)/shard_map/all_gather | solution.py:14
  354.5 0.9 copy-start.30
  355.7 9.4 %copy-start.11 = (bf16[2,128,6,128]{1,0,3,2:T(2,128)(2,1)}, bf16[2,128,6,128]{1,0,3,2:T(2,128)(2,1)S(1)}, u32[]{:S(2)}) copy-start(bf16[2,128,6,128]{1,0,3,2:T(2,128)(2,1)S(1)} %reshape.159) | copy-start | bytes 1179652
  355.7 9.7 %copy-start.4 = (bf16[2048,2,128,1]{0,2,3,1:T(8,128)(2,1)S(1)}, bf16[2048,2,128,1]{0,2,3,1:T(8,128)(2,1)}, u32[]{:S(2)}) copy-start(bf16[2048,2,128,1]{0,2,3,1:T(8,128)(2,1)} %copy.216) | copy-start | bytes 3145732
  361.2 8.1 %copy-start.33 = (f32[6]{0:T(128)}, f32[6]{0:T(128)S(1)}, u32[]{:S(2)}) copy-start(f32[6]{0:T(128)S(1)} %get-tuple-element.345) | copy-start | bytes 76
  363.3 0.9 copy-start.8
  365.1 326.8 %all-reduce.4.cloned.1.call-start = ((), (), s32[]{:S(2)}) async-start(), calls=%async_computation.8 | async-start | bytes 12582912 | tf_op jit(solution)/shard_map/psum | solution.py:251
  369.3 12.9 %copy-start.21 = (bf16[3072,256]{1,0:T(8,128)(2,1)S(1)}, bf16[3072,256]{1,0:T(8,128)(2,1)}, u32[]{:S(2)}) copy-start(bf16[3072,256]{1,0:T(8,128)(2,1)} %param.21) | copy-start | bytes 4718596
  429.6 74.4 %copy-start.27 = (f32[256,256]{0,1:T(8,128)S(1)}, f32[256,256]{0,1:T(8,128)}, u32[]{:S(2)}) copy-start(f32[256,256]{0,1:T(8,128)} %reduce-scatter.5.cloned.1.call-done) | copy-start | bytes 786436
  429.6 69.7 %collective-permute-start.2 = (f32[256,3072]{1,0:T(8,128)S(1)}, f32[256,3072]{1,0:T(8,128)S(1)}, u32[]{:S(2)}, u32[]{:S(2)}) collective-permute-start(f32[256,3072]{1,0:T(8,128)S(1)} %convolution_add_fusion), channel_id=1, source_target_pairs={{0,1},{1,0},{2,3},{3,2},{4,5},{5,4},{6,7},{7,6},{8,9},{9,8},{10,11... | collective-permute-start | bytes 9437192 | tf_op jit(solution)/shard_map/ppermute | solution.py:174
  501.5 4.7 copy-start.26
  501.5 137.5 %collective-permute-start.3 = (f32[256,3072]{1,0:T(8,128)}, f32[256,3072]{1,0:T(8,128)}, u32[]{:S(2)}, u32[]{:S(2)}) collective-permute-start(f32[256,3072]{1,0:T(8,128)} %add.186), channel_id=1, source_target_pairs={{0,2},{1,3},{2,0},{3,1},{4,6},{5,7},{6,4},{7,5},{8,10},{9,11},{10,... | collective-permute-start | bytes 9437192 | tf_op jit(solution)/shard_map/ppermute | solution.py:174
  508.5 130.5 %copy-start.6 = (bf16[256,3072]{1,0:T(8,128)(2,1)S(1)}, bf16[256,3072]{1,0:T(8,128)(2,1)}, u32[]{:S(2)}) copy-start(bf16[256,3072]{1,0:T(8,128)(2,1)} %copy-done.5) | copy-start | bytes 4718596
  508.5 195.6 %all-gather.12.cloned.1.call-start = ((), (), s32[]{:S(2)}) async-start(), calls=%async_computation.5 | async-start | bytes 3538944 | tf_op jit(solution)/shard_map/all_gather | solution.py:14
  642.6 1.1 copy-start.18
  643.7 4.6 copy-start.13
  647.7 2.1 copy-start.35
  647.7 2.1 copy-start.36
  648.3 2.4 copy-start.19
  648.9 0.9 copy-start.7
  669.0 0.6 copy-start.31
  702.6 0.7 copy-start.22
  704.1 14.2 %copy-start.34 = (f32[6]{0:T(128)S(1)}, f32[6]{0:T(128)}, u32[]{:S(2)}) copy-start(f32[6]{0:T(128)} %copy-done.33) | copy-start | bytes 76
  704.1 15.4 %copy-start.12 = (bf16[2,128,6,128]{1,0,3,2:T(2,128)(2,1)S(1)}, bf16[2,128,6,128]{1,0,3,2:T(2,128)(2,1)}, u32[]{:S(2)}) copy-start(bf16[2,128,6,128]{1,0,3,2:T(2,128)(2,1)} %copy-done.11) | copy-start | bytes 1179652
  718.3 2.8 copy-start.23
  719.5 2.2 copy-start.29
Sparse Core Ops, SparseCore 0:
  11.4 26.0 all-gather.7
  39.9 23.3 all-gather.5
  341.1 41.0 reduce-scatter.2
  385.4 41.1 reduce-scatter.4
  428.8 32.1 all-gather.9
  508.6 102.0 all-reduce.3
  650.8 32.1 all-gather.11
